TPU v7x, 32 devices: a whole 2x2x4 slice. The times are simulated.
32 devices in a mesh: frag: 2 (over y), band: 8 (over z, x), slab: 2 (over core).
Axes of the slice: x: 2, y: 2, z: 4, core: 2. Of those that a mesh axis runs over, the one named last changes fastest.
Arguments:
- wavefunctions: bfloat16 [2048, 16384], P('band', ('frag', 'slab')), parts along dimension 1, may hold values from -6 to 6
- eigvec: bfloat16 [2048, 4096], P(None, ('frag', 'band', 'slab')), parts along dimension 1, may hold values from -1 to 1, as said below
- occupation: float32 [4096], P('frag'), parts along dimension 0, may hold values from 0.1 to 2
Outputs:
- rotated: float32 [2048, 16384], P('band', ('frag', 'slab')), parts along dimension 1
- density: float32 [16384], P(('frag', 'slab')), parts along dimension 0
There are 2 independent parts, one for each index of `frag`. A program takes and returns all parts, laid end to end along the dimension named above; each array names one. Nothing has to cross between parts.
Inputs may be any that keep to these rules, and one draw needn't show every extreme that they name: eigvec is an orthogonal matrix rounded to bfloat16.
All inputs are finite; a program needn't handle non-finite values.
Results may differ from a plain program's by a relative error of at most 0.0003.
Values may be sent and summed in bfloat16 or wider, within the bound.
A program may use at most 64 MiB of HBM per device.

v0:
```python
import functools

import jax
import jax.numpy as jnp
from jax import lax
from jax.experimental import pallas as pl
from jax.experimental.pallas import tpu as pltpu
from jax.sharding import PartitionSpec as P

MESH = pl.DeviceIdType.MESH
LANES = 128
AHEAD = 10


def plain(wavefunctions, eigvec, occupation):
    total_bands = eigvec.shape[0]
    by_points = lax.all_to_all(wavefunctions, "band", split_axis=1, concat_axis=0, tiled=True)
    point_rows = lax.dot_general(
        lax.all_gather(eigvec, ("band", "slab"), axis=1, tiled=True),
        by_points,
        (((0,), (0,)), ((), ())),
        preferred_element_type=jnp.float32,
    )
    rotated = lax.all_to_all(point_rows, "band", split_axis=0, concat_axis=1, tiled=True)
    local_density = jnp.dot(
        occupation,
        point_rows * point_rows,
        precision=lax.Precision.HIGHEST,
        preferred_element_type=jnp.float32,
    ) / jnp.float32(total_bands)
    density = lax.all_gather(local_density, "band", axis=0, tiled=True)
    return (rotated, density)


def kernel(nb, wave, panel, weight, out, density, gathered, vectors, staged, part, parts, zrecv, up, down, xrecv, xsend, own, erecv, esend, orecv, osend, drecv, dsend):
    nz = nb // 2
    frag, band, slab = (lax.axis_index(name) for name in ("frag", "band", "slab"))
    z, x = band // 2, lax.rem(band, 2)
    rows, points = wave.shape
    half = points // 2
    steps = half // LANES
    width = panel.shape[0]
    total_bands = panel.shape[1]

    def at(b, s=slab):
        return (frag, b, s)

    beside = 2 * z + 1 - x
    above, below = lax.rem(band + 2, nb), lax.rem(band + nb - 2, nb)

    barrier = pltpu.get_barrier_semaphore()
    for hop in range(1, nb):
        pl.semaphore_signal(barrier, inc=1, device_id=at(lax.rem(band + hop, nb)), device_id_type=MESH)
    for target in (at(band, 1 - slab), at(beside, 1 - slab)):
        pl.semaphore_signal(barrier, inc=1, device_id=target, device_id_type=MESH)
    pl.semaphore_wait(barrier, nb + 1)

    def send(src, dst, ssem, rsem, target):
        return pltpu.make_async_remote_copy(
            src_ref=src, dst_ref=dst, send_sem=ssem, recv_sem=rsem, device_id=target, device_id_type=MESH
        )

    def columns(of, step):
        return pl.ds(pl.multiple_of(of * half + step * LANES, LANES), LANES)

    mine = vectors.at[pl.ds(pl.multiple_of((2 * x + slab) * width, width), width)]

    def vector_copy(i, target):
        return send(panel, mine, esend.at[i], erecv.at[2 * x + slab], target)

    def vector_from(x2, s2):
        there = vectors.at[pl.ds(pl.multiple_of((2 * x2 + s2) * width, width), width)]
        return send(there, there, esend.at[0], erecv.at[2 * x2 + s2], at(band, 1 - slab))

    def across(step):
        return send(wave.at[:, columns(1 - x, step)], gathered.at[step, band], xsend.at[step], xrecv.at[step], at(beside))

    def across_from(step):
        there = gathered.at[step, beside]
        return send(there, there, xsend.at[step], xrecv.at[step], at(beside))

    def keep(step):
        return pltpu.make_async_copy(wave.at[:, columns(x, step)], gathered.at[step, band], own.at[step])

    def pair(step, origin, sems, target):
        both = gathered.at[step, pl.ds(2 * origin, 2)]
        return send(both, both, sems.at[step, origin], zrecv.at[step, origin], at(target))

    def result(step):
        return send(staged.at[step], out.at[:, columns(x, step)], osend.at[step], orecv.at[step], at(beside))

    def result_from(step):
        there = out.at[:, columns(1 - x, step)]
        return send(there, there, osend.at[step], orecv.at[step], at(beside))

    copies = [
        vector_copy(0, at(band, 1 - slab)),
        vector_copy(1, at(beside)),
    ]
    passed = vectors.at[pl.ds(pl.multiple_of((2 * (1 - x) + slab) * width, width), width)]
    relay = send(passed, passed, esend.at[2], erecv.at[2 * (1 - x) + slab], at(band, 1 - slab))

    def begin(step, _):
        across(step).start()
        keep(step).start()
        return _

    lax.fori_loop(0, AHEAD, begin, 0)
    for copy in copies:
        copy.start()
    home = pltpu.make_async_copy(panel, mine, own.at[steps])
    home.start()
    lax.fori_loop(AHEAD, steps, begin, 0)

    def spread(step):
        keep(step).wait()
        across_from(step).wait_recv()

        @pl.when(z < nz - 1)
        def _():
            pair(step, z, up, above).start()

        @pl.when(z > 0)
        def _():
            pair(step, z, down, below).start()

    def collect(step):
        for distance in range(1, nz):
            @pl.when(z + distance < nz)
            def _():
                pair(step, z + distance, down, above).wait_recv()

                @pl.when(z > 0)
                def _():
                    pair(step, z + distance, down, below).start()

            @pl.when(z - distance >= 0)
            def _():
                pair(step, z - distance, up, below).wait_recv()

                @pl.when(z < nz - 1)
                def _():
                    pair(step, z - distance, up, above).start()

    def compute(step):
        block = gathered[step].reshape(nb * rows, LANES)
        here, there = rows * x, rows * (1 - x)
        kept = jnp.dot(vectors[pl.ds(pl.multiple_of(here, rows), rows), :], block, preferred_element_type=jnp.float32)
        sent = jnp.dot(vectors[pl.ds(pl.multiple_of(there, rows), rows), :], block, preferred_element_type=jnp.float32)
        staged[step] = sent
        out[:, columns(x, step)] = kept
        sums = jnp.sum(weight[pl.ds(pl.multiple_of(here, rows), rows), :] * kept * kept, axis=0, keepdims=True)
        sums = sums + jnp.sum(weight[pl.ds(pl.multiple_of(there, rows), rows), :] * sent * sent, axis=0, keepdims=True)
        part[0, :, pl.ds(pl.multiple_of(step * LANES, LANES), LANES)] = sums
        result(step).start()

    def first(step, carry):
        spread(step)
        return carry

    lax.fori_loop(0, AHEAD, first, 0)
    home.wait()
    vector_from(1 - x, slab).wait_recv()
    relay.start()
    vector_from(x, 1 - slab).wait_recv()
    vector_from(1 - x, 1 - slab).wait_recv()

    def body(step, carry):
        @pl.when(step + AHEAD < steps)
        def _():
            spread(step + AHEAD)

        collect(step)
        compute(step)
        return carry

    lax.fori_loop(0, steps, body, 0)

    def share(hop):
        target = lax.rem(band + hop, nb)
        return send(part.at[0], parts.at[band], dsend.at[hop], drecv.at[band], at(target))

    for hop in range(1, nb):
        share(hop).start()
    parts[band] = part[0]

    def finish(step, carry):
        result_from(step).wait_recv()
        result(step).wait_send()
        across(step).wait_send()
        for origin in range(nz):
            @pl.when((z < nz - 1) & (origin <= z))
            def _():
                pair(step, origin, up, above).wait_send()

            @pl.when((z > 0) & (origin >= z))
            def _():
                pair(step, origin, down, below).wait_send()

        return carry

    lax.fori_loop(0, steps, finish, 0)
    for copy in (*copies, relay):
        copy.wait_send()
    for hop in range(1, nb):
        share(hop).wait_send()
        source = lax.rem(band + nb - hop, nb)
        send(parts.at[source], parts.at[source], dsend.at[hop], drecv.at[source], at(source)).wait_recv()
    for side in range(2):
        total = parts[side]
        for level in range(1, nz):
            total = total + parts[2 * level + side]
        density[side] = total / jnp.float32(total_bands)


def local(nb, wavefunctions, eigvec, occupation):
    rows, points = wavefunctions.shape
    total_bands, width = eigvec.shape
    if nb % 2 or width % LANES or rows != 2 * width or points % (2 * LANES) or points // 2 // LANES <= AHEAD:
        return plain(wavefunctions, eigvec, occupation)
    nz, half = nb // 2, points // 2
    steps = half // LANES
    weights = lax.dynamic_slice(occupation, (lax.axis_index("band") // 2 * (2 * rows),), (2 * rows,))
    weights = jnp.broadcast_to(weights[:, None], (2 * rows, LANES))
    vmem = pl.BlockSpec(memory_space=pltpu.VMEM)
    dma = pltpu.SemaphoreType.DMA
    rotated, density = pl.pallas_call(
        functools.partial(kernel, nb),
        out_shape=(
            jax.ShapeDtypeStruct((rows, points), jnp.float32),
            jax.ShapeDtypeStruct((2, 1, half), jnp.float32),
        ),
        in_specs=[vmem] * 3,
        out_specs=(vmem, vmem),
        scratch_shapes=[
            pltpu.VMEM((steps, nb, rows, LANES), jnp.bfloat16),
            pltpu.VMEM((2 * rows, total_bands), jnp.bfloat16),
            pltpu.VMEM((steps, rows, LANES), jnp.float32),
            pltpu.VMEM((1, 1, half), jnp.float32),
            pltpu.VMEM((nb, 1, half), jnp.float32),
            dma((steps, nz)),
            dma((steps, nz)),
            dma((steps, nz)),
            dma((steps,)),
            dma((steps,)),
            dma((steps + 1,)),
            dma((4,)),
            dma((3,)),
            dma((steps,)),
            dma((steps,)),
            dma((nb,)),
            dma((nb,)),
        ],
        compiler_params=pltpu.CompilerParams(
            collective_id=0, has_side_effects=True, vmem_limit_bytes=56 * 2**20
        ),
    )(wavefunctions, eigvec.T, weights)
    return (rotated, density.reshape(points))


def solution(mesh):
    placed = (P("band", ("frag", "slab")), P(None, ("frag", "band", "slab")), P("frag"))
    return jax.shard_map(
        functools.partial(local, mesh.shape["band"]),
        mesh=mesh,
        in_specs=placed,
        out_specs=(P("band", ("frag", "slab")), P(("frag", "slab"))),
        check_vma=False,
    )
```

profile of v0, /device:TPU:0, one launch (start us, length us, event | category | flops | bytes accessed | tf_op | source)
XLA Modules:
  0.0 167.0 jit_solution(14705750684276504776)
XLA Ops:
  0.6 0.8 dynamic_slice.3
  1.4 0.8 broadcast_in_dim.2.weight
  2.2 2.0 %copy.5 = bf16[2048,128]{0,1:T(8,128)(2,1)} copy(bf16[2048,128]{1,0:T(8,128)(2,1)} %param.4) | data formatting | bytes 1048576 | tf_op args[1]
  4.3 157.5 %shard_map.50 = (f32[256,4096]{1,0:T(8,128)}, f32[2,1,2048]{2,1,0:T(1,128)}) custom-call(bf16[256,4096]{1,0:T(8,128)(2,1)} %wave.1, bf16[128,2048]{1,0:T(8,128)(2,1)} %bitcast.2, f32[512,128]{1,0:T(8,128)} %broadcast_in_dim.2.weight), custom_call_target="tpu_custom_call" | custom-call | tf_op jit(solution)/shard_map/pallas_call | solution.py:227
  161.8 0.0 copy-start
  161.8 4.7 %copy.8 = f32[256,4096]{1,0:T(8,128)} copy(f32[256,4096]{1,0:T(8,128)} %get-tuple-element.8) | data formatting | bytes 8388608
  166.4 0.0 copy-done
  166.4 0.6 copy.9
Async XLA Ops:
  161.8 4.7 %copy-start = (f32[2,1,2048]{2,1,0:T(1,128)S(1)}, f32[2,1,2048]{2,1,0:T(1,128)}, u32[]{:S(2)}) copy-start(f32[2,1,2048]{2,1,0:T(1,128)} %get-tuple-element.5) | copy-start | bytes 49156
where the time goes:
time: 167 us
  Pallas kernels  157 us (94%)
  local copies, waits for them, and re-layouts  8.91 us (5%)
    pallas_call x1, Pallas kernels, local(): pl.pallas_call(functools.partial(kernel, nb), out_shape=(jax.ShapeDtypeSt...  157 us
    unnamed x5, local copies, waits for them, and re-layouts  7.31 us

commit v1 on v0

v1 whole, which is shorter than its diff:
```python
import functools

import jax
import jax.numpy as jnp
from jax import lax
from jax.experimental import pallas as pl
from jax.experimental.pallas import tpu as pltpu
from jax.sharding import PartitionSpec as P

MESH = pl.DeviceIdType.MESH
LANES = 128
SHARED = 2


def plain(wavefunctions, eigvec, occupation):
    total_bands = eigvec.shape[0]
    by_points = lax.all_to_all(wavefunctions, "band", split_axis=1, concat_axis=0, tiled=True)
    point_rows = lax.dot_general(
        lax.all_gather(eigvec, ("band", "slab"), axis=1, tiled=True),
        by_points,
        (((0,), (0,)), ((), ())),
        preferred_element_type=jnp.float32,
    )
    rotated = lax.all_to_all(point_rows, "band", split_axis=0, concat_axis=1, tiled=True)
    local_density = jnp.dot(
        occupation,
        point_rows * point_rows,
        precision=lax.Precision.HIGHEST,
        preferred_element_type=jnp.float32,
    ) / jnp.float32(total_bands)
    density = lax.all_gather(local_density, "band", axis=0, tiled=True)
    return (rotated, density)


def kernel(
    wave, eigvec, occupation, out, density,
    gathered, away, raw, vectors, seats, weight, staged, passing, part, parts,
    own_in, away_in, raw_in, seats_in, arrive, away_out, peer_out, mate_out, share_out,
    vec_in, vec_core, vec_side, vec_mate, res_mate, pass_in, mate_in, side_in, side_out, part_out, part_in,
):
    nb, nz = gathered.shape[1], gathered.shape[1] // 2
    frag, band, slab = (lax.axis_index(name) for name in ("frag", "band", "slab"))
    z, x = band // 2, lax.rem(band, 2)
    end = z // 2
    inner = (z == 1) | (z == 2)
    outer = (z == 0) | (z == 3)
    rows, points = wave.shape
    half = points // 2
    steps = half // LANES
    total_bands, width = eigvec.shape
    deep = total_bands // nz
    tall = rows // 2
    ahead = SHARED

    mate_z = 4 * end + 1 - z
    beside = band + 1 - 2 * x
    mate, mate_beside = 2 * mate_z + x, 2 * mate_z + 1 - x
    peer, peer_beside = 2 * (3 - z) + x, 2 * (3 - z) + 1 - x
    far, far_beside = 2 * (3 - mate_z) + x, 2 * (3 - mate_z) + 1 - x

    def at(b, s=slab):
        return (frag, b, s)

    def send(src, dst, ssem, rsem, target):
        return pltpu.make_async_remote_copy(
            src_ref=src, dst_ref=dst, send_sem=ssem, recv_sem=rsem, device_id=target, device_id_type=MESH
        )

    def columns(of, step):
        return pl.ds(pl.multiple_of(of * half + step * LANES, LANES), LANES)

    def own_load(step):
        return pltpu.make_async_copy(wave.at[:, columns(x, step)], gathered.at[step, band], own_in.at[step])

    def away_load(step):
        return pltpu.make_async_copy(wave.at[:, columns(1 - x, step)], away.at[step], away_in.at[step])

    def raw_load(q):
        piece = pl.ds(q * deep, deep)
        return pltpu.make_async_copy(eigvec.at[piece], raw.at[piece], raw_in.at[q])

    seats_load = pltpu.make_async_copy(occupation, seats, seats_in.at[0])

    def across(step):
        return send(away.at[step], gathered.at[step, band], away_out.at[step], arrive.at[step, band], at(beside))

    def block(step, b, sem, target):
        there = gathered.at[step, b]
        return send(there, there, sem, arrive.at[step, b], at(target))

    def arrived(step, b):
        block(step, b, away_out.at[step], beside).wait_recv()

    def seat_of(b):
        return b - 4 * end

    def panel(b, s, q, sem, target):
        seat = seat_of(b) * 2 + s
        there = vectors.at[q, pl.ds(pl.multiple_of(seat * width, width), width)]
        return send(there, there, sem, vec_in.at[seat, q], target)

    def to_core(which, b, q):
        return panel(b, slab, q, vec_core.at[which, q], at(band, 1 - slab))

    def to_side(which, b, q):
        return panel(b, slab, q, vec_side.at[which, q], at(beside))

    def to_mate(q):
        return panel(band, slab, q, vec_mate.at[q], at(mate))

    def panel_wait(b, s, q):
        panel(b, s, q, vec_core.at[0, q], at(beside)).wait_recv()

    def tile(p):
        return pl.ds(p * tall, tall)

    def to_pass(step, p):
        return send(staged.at[step, 0, tile(p)], passing.at[step, tile(p)], res_mate.at[step, p], pass_in.at[step, p], at(mate))

    def to_mate_out(step, p):
        there = out.at[tile(p), columns(x, step)]
        return send(staged.at[step, 1, tile(p)], there, res_mate.at[step, 2 + p], mate_in.at[step, p], at(mate))

    def to_side_out(src, step, p):
        return send(src, out.at[tile(p), columns(x, step)], side_out.at[step, p], side_in.at[step, p], at(beside))

    def from_side_out(step, p):
        there = out.at[tile(p), columns(1 - x, step)]
        send(there, there, side_out.at[step, p], side_in.at[step, p], at(beside)).wait_recv()

    def product(step, b):
        first = pl.multiple_of(seat_of(b) * rows, rows)
        total = None
        for q in range(nz):
            term = jnp.dot(
                vectors[q, pl.ds(first, rows), :],
                gathered[step, pl.ds(2 * q, 2)].reshape(deep, LANES),
                preferred_element_type=jnp.float32,
            )
            total = term if total is None else total + term
        part[step] = part[step] + jnp.sum(weight[pl.ds(first, rows), :] * total * total, axis=0, keepdims=True)
        return total

    def load(step, carry):
        away_load(step).start()
        own_load(step).start()
        return carry

    lax.fori_loop(0, 4, load, 0)
    for q in range(nz):
        raw_load(q).start()
    lax.fori_loop(4, steps, load, 0)
    seats_load.start()

    barrier = pltpu.get_barrier_semaphore()
    for target in (at(beside), at(mate), at(band, 1 - slab)):
        pl.semaphore_signal(barrier, inc=1, device_id=target, device_id_type=MESH)

    @pl.when(inner)
    def _():
        pl.semaphore_signal(barrier, inc=1, device_id=at(peer), device_id_type=MESH)
        pl.semaphore_wait(barrier, 4)

    @pl.when(outer)
    def _():
        pl.semaphore_wait(barrier, 3)

    def exchange(step):
        away_load(step).wait()
        across(step).start()

    def turn():
        for q in range(nz):
            raw_load(q).wait()
            first = pl.multiple_of((seat_of(band) * 2 + slab) * width, width)
            vectors[q, pl.ds(first, width), :] = raw[pl.ds(q * deep, deep), :].T

    def weigh():
        seats_load.wait()
        for group in range(8):
            row = seats[pl.ds(pl.multiple_of(8 * end, 8), 8), :][group : group + 1, :]
            weight[pl.ds(group * LANES, LANES), :] = jnp.broadcast_to(row, (LANES, LANES)).T

    part[...] = jnp.zeros(part.shape, part.dtype)

    @pl.when(inner)
    def _():
        def onward(step, b, i):
            block(step, b, peer_out.at[step, i], peer).start()

        def share(step, b, i):
            block(step, b, share_out.at[step, i], mate).start()

        def mine(step, shared=False):
            own_load(step).wait()
            onward(step, band, 0)
            if shared:
                share(step, band, 0)

        def side(step, shared=False):
            arrived(step, beside)
            onward(step, beside, 1)
            if shared:
                share(step, beside, 1)

        def mates(step):
            for i, b in ((2, mate), (3, mate_beside)):
                arrived(step, b)
                onward(step, b, i)

        def fars(step, shared=False):
            for i, b in ((2, peer), (3, peer_beside), (4, far), (5, far_beside)):
                arrived(step, b)
                if shared:
                    share(step, b, i)

        mine(0, True)
        exchange(0)
        mine(1, True)
        exchange(1)
        exchange(2)
        turn()
        for q in range(nz):
            to_core(0, band, q).start()
        for q in range(2):
            to_side(0, band, q).start()
        weigh()
        for step in range(ahead + 1):
            if step > 1:
                mine(step, step < ahead)
            side(step, step < ahead)
            mates(step)
            if 0 < step:
                fars(step - 1, True)
        exchange(3)
        mine(ahead + 1)
        side(ahead + 1)
        exchange(4)
        for q in range(nz):
            panel_wait(mate, slab, q)
            to_side(1, mate, q).start()
            to_core(2, mate, q).start()
            if q == 1:
                mine(ahead + 2)
                side(ahead + 2)
                exchange(5)
        mine(ahead + 3)
        side(ahead + 3)
        exchange(6)
        for q in range(2, nz):
            to_side(0, band, q).start()
        for q in range(nz):
            panel_wait(mate_beside, slab, q)
            to_core(3, mate_beside, q).start()

        def for_mate(step):
            staged[step, 0] = product(step, mate_beside)
            for p in range(2):
                to_pass(step, p).start()
            staged[step, 1] = product(step, mate)
            for p in range(2):
                to_mate_out(step, p).start()

        def for_row(step):
            staged[step, 2] = product(step, beside)
            for p in range(2):
                to_side_out(staged.at[step, 2, tile(p)], step, p).start()
            out[:, columns(x, step)] = product(step, band)

        def body(step, carry):
            @pl.when(step + 1 < steps)
            def _():
                mates(step + 1)

            @pl.when((step >= ahead + 2) & (step + 2 < steps))
            def _():
                mine(step + 2)
                side(step + 2)

            @pl.when(step + 5 < steps)
            def _():
                exchange(step + 5)

            fars(step)

            @pl.when(step == ahead)
            def _():
                for q in range(nz):
                    panel_wait(mate, 1 - slab, q)
                    panel_wait(mate_beside, 1 - slab, q)

            for_mate(step)

            @pl.when(step == ahead)
            def _():
                for q in range(nz):
                    panel_wait(beside, slab, q)
                    to_core(1, beside, q).start()
                for q in range(nz):
                    panel_wait(band, 1 - slab, q)
                    panel_wait(beside, 1 - slab, q)

            for_row(step - ahead)
            return carry

        lax.fori_loop(ahead, steps, body, 0)

        def rest(step, carry):
            for_row(step)
            return carry

        lax.fori_loop(steps - ahead, steps, rest, 0)

    @pl.when(outer)
    def _():
        def up(step, b, i):
            return block(step, b, mate_out.at[step, i], mate)

        def mine(step):
            own_load(step).wait()
            up(step, band, 0).start()

        def side(step):
            arrived(step, beside)
            up(step, beside, 1).start()

        for step in range(ahead + 1):
            exchange(step)
            mine(step)
        turn()
        for step in range(ahead + 1):
            side(step)
        for q in range(nz):
            to_mate(q).start()
        for step in range(ahead + 1, ahead + 6):
            exchange(step)
        for q in range(nz):
            to_side(0, band, q).start()
            to_core(0, band, q).start()

        def begin(step, carry):
            exchange(step)
            return carry

        lax.fori_loop(ahead + 6, steps, begin, 0)
        weigh()
        for step in range(ahead + 1, ahead + 6):
            mine(step)
            side(step)
        for q in range(nz):
            panel_wait(beside, slab, q)
            to_core(1, beside, q).start()
        for q in range(nz):
            panel_wait(band, 1 - slab, q)
            panel_wait(beside, 1 - slab, q)
        for step in range(ahead):
            for b in (mate, mate_beside, peer, peer_beside, far, far_beside):
                arrived(step, b)
            staged[step, 2] = product(step, beside)
            for p in range(2):
                to_side_out(staged.at[step, 2, tile(p)], step, p).start()
            out[:, columns(x, step)] = product(step, band)

        def body(step, carry):
            @pl.when(step + 6 < steps)
            def _():
                mine(step + 6)
                side(step + 6)

            for p in range(2):
                to_pass(step, p).wait_recv()
                to_side_out(passing.at[step, tile(p)], step, p).start()
            return carry

        lax.fori_loop(ahead, steps, body, 0)

    def spread(hop):
        target = lax.rem(band + hop, nb)
        return send(part, parts.at[band], part_out.at[hop], part_in.at[band], at(target))

    for hop in range(1, nb):
        spread(hop).start()
    parts[band] = part[...]
    for hop in range(1, nb):
        source = lax.rem(band + nb - hop, nb)
        send(parts.at[source], parts.at[source], part_out.at[hop], part_in.at[source], at(source)).wait_recv()
    for of in range(2):
        total = parts[of]
        for level in range(1, nz):
            total = total + parts[2 * level + of]
        density[of] = total / jnp.float32(total_bands)

    def finish(step, carry):
        across(step).wait_send()
        for p in range(2):
            to_side_out(passing.at[step, tile(p)], step, p).wait_send()
            from_side_out(step, p)

        @pl.when(inner)
        def _():
            for i, b in enumerate((band, beside, mate, mate_beside)):
                block(step, b, peer_out.at[step, i], peer).wait_send()

            @pl.when(step < ahead)
            def _():
                for i, b in enumerate((band, beside, peer, peer_beside, far, far_beside)):
                    block(step, b, share_out.at[step, i], mate).wait_send()

            @pl.when(step >= ahead)
            def _():
                for p in range(2):
                    to_pass(step, p).wait_send()
                    to_mate_out(step, p).wait_send()

        @pl.when(outer)
        def _():
            for i, b in enumerate((band, beside)):
                block(step, b, mate_out.at[step, i], mate).wait_send()

            @pl.when(step >= ahead)
            def _():
                for p in range(2):
                    there = out.at[tile(p), columns(x, step)]
                    send(there, there, res_mate.at[step, p], mate_in.at[step, p], at(mate)).wait_recv()

        return carry

    lax.fori_loop(0, steps, finish, 0)
    for q in range(nz):
        to_core(0, band, q).wait_send()
        to_core(1, beside, q).wait_send()
        to_side(0, band, q).wait_send()

        @pl.when(inner)
        def _():
            to_core(2, mate, q).wait_send()
            to_core(3, mate_beside, q).wait_send()
            to_side(1, mate, q).wait_send()

        @pl.when(outer)
        def _():
            to_mate(q).wait_send()

    for hop in range(1, nb):
        spread(hop).wait_send()


def local(nb, wavefunctions, eigvec, occupation):
    rows, points = wavefunctions.shape
    total_bands, width = eigvec.shape
    steps = points // 2 // LANES
    if nb != 8 or width != LANES or rows != 2 * width or points % (2 * LANES) or steps < SHARED + 8 or total_bands != nb * rows:
        return plain(wavefunctions, eigvec, occupation)
    nz, deep = nb // 2, total_bands // (nb // 2)
    vmem = pl.BlockSpec(memory_space=pltpu.VMEM)
    hbm = pl.BlockSpec(memory_space=pltpu.HBM)
    dma = pltpu.SemaphoreType.DMA
    rotated, density = pl.pallas_call(
        kernel,
        out_shape=(
            pltpu.VMEM((rows, points), jnp.float32),
            pltpu.VMEM((2, steps, 1, LANES), jnp.float32),
        ),
        in_specs=[hbm] * 3,
        out_specs=(vmem, vmem),
        scratch_shapes=[
            pltpu.VMEM((steps, nb, rows, LANES), jnp.bfloat16),
            pltpu.VMEM((steps, rows, LANES), jnp.bfloat16),
            pltpu.VMEM((total_bands, width), jnp.bfloat16),
            pltpu.VMEM((nz, 4 * rows, deep), jnp.bfloat16),
            pltpu.VMEM((total_bands // LANES, LANES), jnp.float32),
            pltpu.VMEM((4 * rows, LANES), jnp.float32),
            pltpu.VMEM((steps, 3, rows, LANES), jnp.float32),
            pltpu.VMEM((steps, rows, LANES), jnp.float32),
            pltpu.VMEM((steps, 1, LANES), jnp.float32),
            pltpu.VMEM((nb, steps, 1, LANES), jnp.float32),
            dma((steps,)),
            dma((steps,)),
            dma((nz,)),
            dma((1,)),
            dma((steps, nb)),
            dma((steps,)),
            dma((steps, 4)),
            dma((steps, 2)),
            dma((SHARED, 6)),
            dma((8, nz)),
            dma((4, nz)),
            dma((2, nz)),
            dma((nz,)),
            dma((steps, 4)),
            dma((steps, 2)),
            dma((steps, 2)),
            dma((steps, 2)),
            dma((steps, 2)),
            dma((nb,)),
            dma((nb,)),
        ],
        compiler_params=pltpu.CompilerParams(
            collective_id=0, has_side_effects=True, vmem_limit_bytes=56 * 2**20
        ),
    )(wavefunctions, eigvec, occupation.reshape(total_bands // LANES, LANES))
    return (rotated, density.reshape(points))


def solution(mesh):
    placed = (P("band", ("frag", "slab")), P(None, ("frag", "band", "slab")), P("frag"))
    return jax.shard_map(
        functools.partial(local, mesh.shape["band"]),
        mesh=mesh,
        in_specs=placed,
        out_specs=(P("band", ("frag", "slab")), P(("frag", "slab"))),
        check_vma=False,
    )
```

time: 167 us -> 131 us (0.78)
  Pallas kernels: 157 us -> 128 us
  local copies, waits for them, and re-layouts: 8.91 us -> 2.62 us
    pallas_call x1, Pallas kernels: 157 us -> 128 us  [local(): pl.pallas_call(kernel, out_shape=(pltpu.VMEM((rows, points), jnp.float32)...]
    unnamed x5 -> x2, local copies, waits for them, and re-layouts: 7.31 us -> 2.62 us
where the time goes in v1:
time: 131 us
  Pallas kernels  128 us (98%)
  local copies, waits for them, and re-layouts  2.62 us (2%)
    pallas_call x1, Pallas kernels, local(): pl.pallas_call(kernel, out_shape=(pltpu.VMEM((rows, points), jnp.float32)...  128 us
    unnamed x2, local copies, waits for them, and re-layouts  2.62 us

profile of v1, /device:TPU:0, one launch (start us, length us, event | category | flops | bytes accessed | tf_op | source)
XLA Modules:
  0.0 131.3 jit_solution(12397911085359384720)
XLA Ops:
  0.6 128.0 %shard_map.50 = (f32[256,4096]{1,0:T(8,128)S(1)}, f32[2,16,1,128]{3,2,1,0:T(1,128)S(1)}) custom-call(bf16[256,4096]{1,0:T(8,128)(2,1)} %wave.1, bf16[2048,128]{1,0:T(8,128)(2,1)} %eigvec.1, f32[16,128]{1,0:T(8,128)} %bitcast.3), custom_call_target="tpu_custom_call" | custom-call | tf_op jit(solution)/shard_map/pallas_call | solution.py:458
  128.7 2.0 %copy.7 = f32[256,4096]{1,0:T(8,128)} copy(f32[256,4096]{1,0:T(8,128)S(1)} %get-tuple-element.6) | data formatting | bytes 8388608
  130.7 0.6 copy.8

commit v2 on v1

v2 whole, which is shorter than its diff:
```python
import functools

import jax
import jax.numpy as jnp
from jax import lax
from jax.experimental import pallas as pl
from jax.experimental.pallas import tpu as pltpu
from jax.sharding import PartitionSpec as P

MESH = pl.DeviceIdType.MESH
LANES = 128
SHARED = 3


def plain(wavefunctions, eigvec, occupation):
    total_bands = eigvec.shape[0]
    by_points = lax.all_to_all(wavefunctions, "band", split_axis=1, concat_axis=0, tiled=True)
    point_rows = lax.dot_general(
        lax.all_gather(eigvec, ("band", "slab"), axis=1, tiled=True),
        by_points,
        (((0,), (0,)), ((), ())),
        preferred_element_type=jnp.float32,
    )
    rotated = lax.all_to_all(point_rows, "band", split_axis=0, concat_axis=1, tiled=True)
    local_density = jnp.dot(
        occupation,
        point_rows * point_rows,
        precision=lax.Precision.HIGHEST,
        preferred_element_type=jnp.float32,
    ) / jnp.float32(total_bands)
    density = lax.all_gather(local_density, "band", axis=0, tiled=True)
    return (rotated, density)


def kernel(
    wave, eigvec, occupation, out, density,
    gathered, away, raw, vectors, seats, weight, staged, passing, part, parts,
    own_in, away_in, raw_in, seats_in, early, late, away_out, peer_out, mate_out, share_out,
    vec_in, vec_core_in, vec_core, vec_side, vec_mate, res_mate, pass_in, mate_in, side_in, side_out, kept, part_out, part_in,
):
    nb, nz = gathered.shape[1], gathered.shape[1] // 2
    frag, band, slab = (lax.axis_index(name) for name in ("frag", "band", "slab"))
    z, x = band // 2, lax.rem(band, 2)
    end = z // 2
    inner = (z == 1) | (z == 2)
    outer = (z == 0) | (z == 3)
    rows, points = wave.shape
    half = points // 2
    steps = half // LANES
    total_bands, width = eigvec.shape
    deep = total_bands // nz
    tall = rows // 2
    ahead = SHARED

    mate_z = 4 * end + 1 - z
    beside = band + 1 - 2 * x
    mate, mate_beside = 2 * mate_z + x, 2 * mate_z + 1 - x
    peer, peer_beside = 2 * (3 - z) + x, 2 * (3 - z) + 1 - x
    far, far_beside = 2 * (3 - mate_z) + x, 2 * (3 - mate_z) + 1 - x

    def at(b, s=slab):
        return (frag, b, s)

    def send(src, dst, ssem, rsem, target):
        return pltpu.make_async_remote_copy(
            src_ref=src, dst_ref=dst, send_sem=ssem, recv_sem=rsem, device_id=target, device_id_type=MESH
        )

    def columns(of, step):
        return pl.ds(pl.multiple_of(of * half + step * LANES, LANES), LANES)

    def settle(ref, sem):
        pltpu.make_async_copy(ref, ref, sem).wait()

    def own_load(step, i):
        return pltpu.make_async_copy(wave.at[:, columns(x, step)], gathered.at[step, band], own_in.at[i])

    def away_load(step, i):
        return pltpu.make_async_copy(wave.at[:, columns(1 - x, step)], away.at[step], away_in.at[i])

    raw_load = pltpu.make_async_copy(eigvec, raw, raw_in.at[0])
    seats_load = pltpu.make_async_copy(occupation, seats, seats_in.at[0])

    def block(step, b, sem, target, way):
        there = gathered.at[step, b]
        rsem = early.at[step, b] if isinstance(step, int) and step < ahead else late.at[step - ahead, way]
        return send(there, there, sem.at[0], rsem, at(target))

    def across(step):
        rsem = early.at[step, band] if isinstance(step, int) and step < ahead else late.at[step - ahead, 0]
        return send(away.at[step], gathered.at[step, band], away_out.at[0], rsem, at(beside))

    def arrived(step, bands, way):
        if isinstance(step, int) and step < ahead:
            for b in bands:
                settle(gathered.at[step, b], early.at[step, b])
        else:
            settle(gathered.at[step, pl.ds(0, len(bands))], late.at[step - ahead, way])

    def seat_of(b):
        return b - 4 * end

    def panel_at(b, s):
        return pl.ds(pl.multiple_of((seat_of(b) * 2 + s) * width, width), width)

    def to_core(b, q):
        there = vectors.at[q, panel_at(b, slab)]
        return send(there, there, vec_core.at[0], vec_core_in.at[seat_of(b)], at(band, 1 - slab))

    def panel(b, q, sem, target):
        there = vectors.at[q, panel_at(b, slab)]
        return send(there, there, sem.at[0], vec_in.at[seat_of(b), q], at(target))

    def panel_wait(b, q):
        settle(vectors.at[q, panel_at(b, slab)], vec_in.at[seat_of(b), q])

    def core_wait(b):
        settle(vectors.at[:, panel_at(b, 1 - slab)], vec_core_in.at[seat_of(b)])

    def tile(p):
        return pl.ds(p * tall, tall)

    def pass_sem(step, p):
        return pass_in.at[step - ahead + p * (step == steps - 1)]

    def to_pass(step, p):
        return send(staged.at[step, 0, tile(p)], passing.at[step, tile(p)], res_mate.at[0], pass_sem(step, p), at(mate))

    def to_mate_out(step, p):
        there = out.at[tile(p), columns(x, step)]
        return send(staged.at[step, 1, tile(p)], there, res_mate.at[0], mate_in.at[0], at(mate))

    def to_side_out(src, step, p):
        return send(src, out.at[tile(p), columns(x, step)], side_out.at[0], side_in.at[0], at(beside))

    def keep(step):
        return pltpu.make_async_copy(staged.at[step, 3], out.at[:, columns(x, step)], kept.at[0])

    def product(step, b):
        first = pl.multiple_of(seat_of(b) * rows, rows)
        total = None
        for q in range(nz):
            term = jnp.dot(
                vectors[q, pl.ds(first, rows), :],
                gathered[step, pl.ds(2 * q, 2)].reshape(deep, LANES),
                preferred_element_type=jnp.float32,
            )
            total = term if total is None else total + term
        part[step] = part[step] + jnp.sum(weight[pl.ds(first, rows), :] * total * total, axis=0, keepdims=True)
        return total

    def load(step, carry):
        i = step if isinstance(step, int) else ahead + 1
        away_load(step, i).start()
        own_load(step, i).start()
        return carry

    for step in range(ahead + 1):
        load(step, None)
    raw_load.start()
    seats_load.start()

    barrier = pltpu.get_barrier_semaphore()
    for target in (at(beside), at(mate), at(band, 1 - slab)):
        pl.semaphore_signal(barrier, inc=1, device_id=target, device_id_type=MESH)

    @pl.when(inner)
    def _():
        pl.semaphore_signal(barrier, inc=1, device_id=at(peer), device_id_type=MESH)
        pl.semaphore_wait(barrier, 4)

    @pl.when(outer)
    def _():
        pl.semaphore_wait(barrier, 3)

    def exchange(step):
        if isinstance(step, int) and step <= ahead:
            away_load(step, step).wait()
        across(step).start()

    def own_ready(step):
        if isinstance(step, int) and step <= ahead:
            own_load(step, step).wait()

    def rest_ready():
        others = pl.ds(ahead + 1, steps - ahead - 1)
        settle(away.at[others], away_in.at[ahead + 1])
        settle(away.at[others], own_in.at[ahead + 1])

    def turn():
        raw_load.wait()
        for q in range(nz):
            vectors[q, panel_at(band, slab), :] = raw[pl.ds(q * deep, deep), :].T

    def weigh():
        seats_load.wait()
        for group in range(8):
            row = seats[pl.ds(pl.multiple_of(8 * end, 8), 8), :][group : group + 1, :]
            weight[pl.ds(group * LANES, LANES), :] = jnp.broadcast_to(row, (LANES, LANES)).T

    part[...] = jnp.zeros(part.shape, part.dtype)

    def spread(hop):
        target = lax.rem(band + hop, nb)
        return send(part, parts.at[band], part_out.at[0], part_in.at[0], at(target))

    @pl.when(inner)
    def _():
        def onward(step, b):
            block(step, b, peer_out, peer, 2).start()

        def share(step, b):
            if isinstance(step, int) and step < ahead:
                block(step, b, share_out, mate, 1).start()

        def mine(step):
            own_ready(step)
            onward(step, band)
            share(step, band)

        def side(step):
            arrived(step, (beside,), 0)
            onward(step, beside)
            share(step, beside)

        def mates(step, which=(0, 1)):
            bands = [(mate, mate_beside)[i] for i in which]
            arrived(step, bands, 1)
            for b in bands:
                onward(step, b)

        def fars(step, which=(0, 1, 2, 3)):
            bands = [(peer, peer_beside, far, far_beside)[i] for i in which]
            arrived(step, bands, 2)
            for b in bands:
                share(step, b)

        def mate_panel(q):
            panel_wait(mate, q)
            panel(mate, q, vec_side, beside).start()
            to_core(mate, q).start()

        for step in range(ahead):
            mine(step)
            exchange(step)
        exchange(ahead)
        lax.fori_loop(ahead + 1, steps, load, 0)
        turn()
        for q in range(nz):
            to_core(band, q).start()
        rest_ready()
        exchange(4)
        exchange(5)
        for q in range(2):
            panel(band, q, vec_side, beside).start()
        weigh()
        for step in range(ahead):
            side(step)
            mates(step, (0,))
            fars(step, (0,))
        mine(3)
        for step in range(ahead):
            mates(step, (1,))
            fars(step, (1,))
        side(3)
        mates(3)
        mine(4)
        side(4)
        fars(0, (2, 3))
        mate_panel(0)
        fars(1, (2, 3))
        mate_panel(1)
        mine(5)
        side(5)
        fars(2, (2, 3))
        mate_panel(2)
        mate_panel(3)
        exchange(6)
        panel(band, 2, vec_side, beside).start()
        exchange(7)
        panel(band, 3, vec_side, beside).start()

        def for_mate(step):
            first = (step == ahead).astype(jnp.int32)
            for turn_of in range(2):
                slot = first * (1 - turn_of) + (1 - first) * turn_of
                b = 2 * mate_z + slot * x + (1 - slot) * (1 - x)

                @pl.when(step == ahead)
                def _():
                    if turn_of == 1:
                        mates(step + 1)
                        for q in range(nz):
                            panel_wait(mate_beside, q)
                            to_core(mate_beside, q).start()
                    core_wait((mate, mate_beside)[turn_of])

                staged[step, slot] = product(step, b)

                @pl.when(slot == 0)
                def _():
                    for p in range(2):
                        to_pass(step, p).start()

                @pl.when(slot == 1)
                def _():
                    for p in range(2):
                        to_mate_out(step, p).start()

        def for_row(step, carry):
            staged[step, 2] = product(step, beside)
            for p in range(2):
                to_side_out(staged.at[step, 2, tile(p)], step, p).start()
            staged[step, 3] = product(step, band)
            keep(step).start()
            return carry

        lag = ahead + 1

        def rows_done(step):
            return jnp.maximum(step + 1 - lag, 0) + jnp.minimum(jnp.maximum(step - 8, 0), lag)

        def body(step, carry):
            fars(step)
            for_mate(step)

            @pl.when((step > ahead) & (step + 1 < steps))
            def _():
                mates(step + 1)

            @pl.when((step >= 4) & (step + 2 < steps))
            def _():
                mine(step + 2)
                side(step + 2)

            @pl.when(step + 5 < steps)
            def _():
                exchange(step + 5)

            @pl.when(step == lag)
            def _():
                for q in range(nz):
                    panel_wait(beside, q)
                    to_core(beside, q).start()
                core_wait(band)
                core_wait(beside)

            lax.fori_loop(rows_done(step - 1), rows_done(step), for_row, 0)
            return carry

        lax.fori_loop(ahead, steps, body, 0)
        for hop in range(1, nb):
            spread(hop).start()

    @pl.when(outer)
    def _():
        def mine(step):
            own_ready(step)
            block(step, band, mate_out, mate, 1).start()

        def side(step):
            arrived(step, (beside,), 0)
            block(step, beside, mate_out, mate, 1).start()

        for step in range(ahead + 1):
            exchange(step)
            mine(step)
        lax.fori_loop(ahead + 1, steps, load, 0)
        turn()
        rest_ready()
        for step in range(ahead + 1, ahead + 5):
            exchange(step)
        for step in range(ahead + 1):
            side(step)
        for q in range(nz):
            panel(band, q, vec_mate, mate).start()
        for q in range(nz):
            panel(band, q, vec_side, beside).start()
            to_core(band, q).start()

        def begin(step, carry):
            exchange(step)
            return carry

        lax.fori_loop(ahead + 5, steps, begin, 0)
        weigh()
        for step in range(ahead + 1, ahead + 5):
            mine(step)
            side(step)
        for q in range(nz):
            panel_wait(beside, q)
            to_core(beside, q).start()
        core_wait(band)
        core_wait(beside)

        def shared(step, carry):
            for b in (mate, mate_beside, peer, peer_beside, far, far_beside):
                settle(gathered.at[step, b], early.at[step, b])
            staged[step, 2] = product(step, beside)
            for p in range(2):
                to_side_out(staged.at[step, 2, tile(p)], step, p).start()
            staged[step, 3] = product(step, band)
            keep(step).start()
            return carry

        lax.fori_loop(0, ahead, shared, 0)
        for hop in range(1, nb):
            spread(hop).start()

        def body(step, carry):
            @pl.when(step + 5 < steps)
            def _():
                mine(step + 5)
                side(step + 5)

            settle(passing.at[step], pass_in.at[step - ahead])
            for p in range(2):
                to_side_out(passing.at[step, tile(p)], step, p).start()
            return carry

        lax.fori_loop(ahead, steps - 1, body, 0)
        for p in range(2):
            settle(passing.at[steps - 1, tile(p)], pass_in.at[steps - 1 - ahead + p])
            to_side_out(passing.at[steps - 1, tile(p)], steps - 1, p).start()

    parts[band] = part[...]
    others = parts.at[pl.ds(0, nb - 1)]
    settle(others, part_in.at[0])
    for of in range(2):
        total = parts[of]
        for level in range(1, nz):
            total = total + parts[2 * level + of]
        density[of] = total / jnp.float32(total_bands)

    def blocks(n):
        return staged.at[pl.ds(0, n // 2), 0]

    settle(away, away_out.at[0])
    settle(others, part_out.at[0])

    @pl.when(inner)
    def _():
        settle(gathered.at[pl.ds(0, steps // 2)], peer_out.at[0])
        settle(blocks(6 * ahead), share_out.at[0])
        settle(vectors.at[:, pl.ds(0, 4 * width)], vec_core.at[0])
        settle(vectors.at[:, pl.ds(0, 2 * width)], vec_side.at[0])
        settle(staged.at[pl.ds(ahead, steps - ahead), pl.ds(0, 2)], res_mate.at[0])
        settle(blocks(2 * steps), kept.at[0])

    @pl.when(outer)
    def _():
        settle(blocks(2 * steps), mate_out.at[0])
        settle(vectors.at[:, pl.ds(0, 2 * width)], vec_core.at[0])
        settle(vectors.at[:, pl.ds(0, width)], vec_side.at[0])
        settle(vectors.at[:, pl.ds(0, width)], vec_mate.at[0])
        settle(blocks(2 * ahead), kept.at[0])
        settle(blocks(2 * (steps - ahead)), mate_in.at[0])

    settle(blocks(2 * steps), side_out.at[0])
    settle(blocks(2 * steps), side_in.at[0])


def local(nb, wavefunctions, eigvec, occupation):
    rows, points = wavefunctions.shape
    total_bands, width = eigvec.shape
    steps = points // 2 // LANES
    if nb != 8 or width != LANES or rows != 2 * width or points % (2 * LANES) or steps < SHARED + 8 or total_bands != nb * rows:
        return plain(wavefunctions, eigvec, occupation)
    nz, deep = nb // 2, total_bands // (nb // 2)
    vmem = pl.BlockSpec(memory_space=pltpu.VMEM)
    hbm = pl.BlockSpec(memory_space=pltpu.HBM)
    dma = pltpu.SemaphoreType.DMA
    rotated, density = pl.pallas_call(
        kernel,
        out_shape=(
            pltpu.VMEM((rows, points), jnp.float32),
            pltpu.VMEM((2, steps, 1, LANES), jnp.float32),
        ),
        in_specs=[hbm] * 3,
        out_specs=(pl.BlockSpec(memory_space=pl.ANY), vmem),
        scratch_shapes=[
            pltpu.VMEM((steps, nb, rows, LANES), jnp.bfloat16),
            pltpu.VMEM((steps, rows, LANES), jnp.bfloat16),
            pltpu.VMEM((total_bands, width), jnp.bfloat16),
            pltpu.VMEM((nz, 4 * rows, deep), jnp.bfloat16),
            pltpu.VMEM((total_bands // LANES, LANES), jnp.float32),
            pltpu.VMEM((4 * rows, LANES), jnp.float32),
            pltpu.VMEM((steps, 4, rows, LANES), jnp.float32),
            pltpu.VMEM((steps, rows, LANES), jnp.float32),
            pltpu.VMEM((steps, 1, LANES), jnp.float32),
            pltpu.VMEM((nb, steps, 1, LANES), jnp.float32),
            dma((SHARED + 2,)),
            dma((SHARED + 2,)),
            dma((1,)),
            dma((1,)),
            dma((SHARED, nb)),
            dma((steps - SHARED, 3)),
            *[dma((1,))] * 4,
            dma((4, nz)),
            dma((4,)),
            *[dma((1,))] * 4,
            dma((steps - SHARED + 1,)),
            *[dma((1,))] * 6,
        ],
        compiler_params=pltpu.CompilerParams(
            collective_id=0, has_side_effects=True, vmem_limit_bytes=56 * 2**20
        ),
    )(wavefunctions, eigvec, occupation.reshape(total_bands // LANES, LANES))
    return (rotated, density.reshape(points))


def solution(mesh):
    placed = (P("band", ("frag", "slab")), P(None, ("frag", "band", "slab")), P("frag"))
    return jax.shard_map(
        functools.partial(local, mesh.shape["band"]),
        mesh=mesh,
        in_specs=placed,
        out_specs=(P("band", ("frag", "slab")), P(("frag", "slab"))),
        check_vma=False,
    )
```

time: 131 us -> 117 us (0.89)
  Pallas kernels: 128 us -> 114 us
    pallas_call x1, Pallas kernels: 128 us -> 114 us  [local(): pl.pallas_call(kernel, out_shape=(pltpu.VMEM((rows, points), jnp.float32)...]
where the time goes in v2:
time: 117 us
  Pallas kernels  114 us (97%)
  local copies, waits for them, and re-layouts  2.62 us (2%)
    pallas_call x1, Pallas kernels, local(): pl.pallas_call(kernel, out_shape=(pltpu.VMEM((rows, points), jnp.float32)...  114 us
    unnamed x2, local copies, waits for them, and re-layouts  2.62 us

profile of v2, /device:TPU:0, one launch (start us, length us, event | category | flops | bytes accessed | tf_op | source)
XLA Modules:
  0.0 116.9 jit_solution(6377611526335250556)
XLA Ops:
  0.6 113.6 %shard_map.50 = (f32[256,4096]{1,0:T(8,128)S(1)}, f32[2,16,1,128]{3,2,1,0:T(1,128)S(1)}) custom-call(bf16[256,4096]{1,0:T(8,128)(2,1)} %wave.1, bf16[2048,128]{1,0:T(8,128)(2,1)} %eigvec.1, f32[16,128]{1,0:T(8,128)} %bitcast.3), custom_call_target="tpu_custom_call" | custom-call | tf_op jit(solution)/shard_map/pallas_call | solution.py:473
  114.3 2.0 %copy.7 = f32[256,4096]{1,0:T(8,128)} copy(f32[256,4096]{1,0:T(8,128)S(1)} %get-tuple-element.6) | data formatting | bytes 8388608
  116.3 0.6 copy.8

commit v3 on v2

--- a/solution.py
+++ b/solution.py
@@ -249,10 +249,9 @@
         for q in range(nz):
             to_core(band, q).start()
         rest_ready()
-        exchange(4)
-        exchange(5)
-        for q in range(2):
-            panel(band, q, vec_side, beside).start()
+        for step in range(4, 8):
+            exchange(step)
+        panel(band, 0, vec_side, beside).start()
         weigh()
         for step in range(ahead):
             side(step)
@@ -275,10 +274,6 @@
         fars(2, (2, 3))
         mate_panel(2)
         mate_panel(3)
-        exchange(6)
-        panel(band, 2, vec_side, beside).start()
-        exchange(7)
-        panel(band, 3, vec_side, beside).start()
 
         def for_mate(step):
             first = (step == ahead).astype(jnp.int32)
@@ -290,10 +285,16 @@
                 def _():
                     if turn_of == 1:
                         mates(step + 1)
+                        mine(step + 3)
+                        side(step + 3)
                         for q in range(nz):
                             panel_wait(mate_beside, q)
                             to_core(mate_beside, q).start()
                     core_wait((mate, mate_beside)[turn_of])
+                    if turn_of == 1:
+                        exchange(step + 5)
+                        for q in range(1, nz):
+                            panel(band, q, vec_side, beside).start()
 
                 staged[step, slot] = product(step, b)
 
@@ -315,25 +316,25 @@
             keep(step).start()
             return carry
 
-        lag = ahead + 1
+        lag = ahead + 2
 
         def rows_done(step):
-            return jnp.maximum(step + 1 - lag, 0) + jnp.minimum(jnp.maximum(step - 8, 0), lag)
+            return jnp.maximum(step + 1 - lag, 0) + jnp.minimum(jnp.maximum(step - 4, 0) // 2, lag)
 
         def body(step, carry):
             fars(step)
             for_mate(step)
 
-            @pl.when((step > ahead) & (step + 1 < steps))
+            @pl.when((step > ahead) & (step + 3 < steps))
             def _():
-                mates(step + 1)
-
-            @pl.when((step >= 4) & (step + 2 < steps))
+                mine(step + 3)
+                side(step + 3)
+
+            @pl.when(step + 2 < steps)
             def _():
-                mine(step + 2)
-                side(step + 2)
-
-            @pl.when(step + 5 < steps)
+                mates(step + 2)
+
+            @pl.when((step > ahead) & (step + 5 < steps))
             def _():
                 exchange(step + 5)
 

time: 117 us -> 114 us (0.974)
  Pallas kernels: 114 us -> 110 us
    pallas_call x1, Pallas kernels: 114 us -> 110 us  [local(): pl.pallas_call(kernel, out_shape=(pltpu.VMEM((rows, points), jnp.float32)...]
where the time goes in v3:
time: 114 us
  Pallas kernels  110 us (96%)
  local copies, waits for them, and re-layouts  2.62 us (2%)
    pallas_call x1, Pallas kernels, local(): pl.pallas_call(kernel, out_shape=(pltpu.VMEM((rows, points), jnp.float32)...  110 us
    unnamed x2, local copies, waits for them, and re-layouts  2.62 us

profile of v3, /device:TPU:0, one launch (start us, length us, event | category | flops | bytes accessed | tf_op | source)
XLA Modules:
  0.0 113.8 jit_solution(15704475404239022779)
XLA Ops:
  0.6 110.5 %shard_map.50 = (f32[256,4096]{1,0:T(8,128)S(1)}, f32[2,16,1,128]{3,2,1,0:T(1,128)S(1)}) custom-call(bf16[256,4096]{1,0:T(8,128)(2,1)} %wave.1, bf16[2048,128]{1,0:T(8,128)(2,1)} %eigvec.1, f32[16,128]{1,0:T(8,128)} %bitcast.3), custom_call_target="tpu_custom_call" | custom-call | tf_op jit(solution)/shard_map/pallas_call | solution.py:474
  111.1 2.0 %copy.7 = f32[256,4096]{1,0:T(8,128)} copy(f32[256,4096]{1,0:T(8,128)S(1)} %get-tuple-element.6) | data formatting | bytes 8388608
  113.1 0.6 copy.8

commit v4 on v3

--- a/solution.py
+++ b/solution.py
@@ -9,6 +9,7 @@
 
 MESH = pl.DeviceIdType.MESH
 LANES = 128
+PIECES = 8
 SHARED = 3
 
 
@@ -303,7 +304,7 @@
                     for p in range(2):
                         to_pass(step, p).start()
 
-                @pl.when(slot == 1)
+                @pl.when((slot == 1) & (step < steps - 2))
                 def _():
                     for p in range(2):
                         to_mate_out(step, p).start()
@@ -352,6 +353,9 @@
         lax.fori_loop(ahead, steps, body, 0)
         for hop in range(1, nb):
             spread(hop).start()
+        for step in (steps - 2, steps - 1):
+            for p in range(2):
+                to_mate_out(step, p).start()
 
     @pl.when(outer)
     def _():
@@ -459,6 +463,19 @@
 
     settle(blocks(2 * steps), side_out.at[0])
     settle(blocks(2 * steps), side_in.at[0])
+
+
+def flush(rotated, density, rotated_out, density_out, sems):
+    band = rotated.shape[0] // PIECES
+    copies = [
+        pltpu.make_async_copy(rotated.at[pl.ds(i * band, band)], rotated_out.at[pl.ds(i * band, band)], sems.at[i])
+        for i in range(PIECES)
+    ]
+    copies.append(pltpu.make_async_copy(density, density_out, sems.at[PIECES]))
+    for copy in copies:
+        copy.start()
+    for copy in copies:
+        copy.wait()
 
 
 def local(nb, wavefunctions, eigvec, occupation):
@@ -507,6 +524,17 @@
             collective_id=0, has_side_effects=True, vmem_limit_bytes=56 * 2**20
         ),
     )(wavefunctions, eigvec, occupation.reshape(total_bands // LANES, LANES))
+    rotated, density = pl.pallas_call(
+        flush,
+        out_shape=(
+            jax.ShapeDtypeStruct(rotated.shape, rotated.dtype),
+            jax.ShapeDtypeStruct(density.shape, density.dtype),
+        ),
+        in_specs=[pl.BlockSpec(memory_space=pl.ANY)] * 2,
+        out_specs=(hbm, hbm),
+        scratch_shapes=[dma((PIECES + 1,))],
+        compiler_params=pltpu.CompilerParams(vmem_limit_bytes=2**20),
+    )(rotated, density)
     return (rotated, density.reshape(points))
 
 

time: 114 us -> 112 us (0.982)
  local copies, waits for them, and re-layouts: 2.62 us -> 0 us
    unnamed x2 -> x0, local copies, waits for them, and re-layouts: 2.62 us -> none
    pallas_call x0 -> x1, Pallas kernels: none -> 2.08 us  [local(): pl.pallas_call(flush, out_shape=(jax.ShapeDtypeStruct(rotated.shape, rota...]
    pallas_call x1, Pallas kernels: 110 us -> 109 us  [local(): pl.pallas_call(kernel, out_shape=(pltpu.VMEM((rows, points), jnp.float32)...]
where the time goes in v4:
time: 112 us
  Pallas kernels  111 us (99%)
    pallas_call x1, Pallas kernels, local(): pl.pallas_call(kernel, out_shape=(pltpu.VMEM((rows, points), jnp.float32)...  109 us

profile of v4, /device:TPU:0, one launch (start us, length us, event | category | flops | bytes accessed | tf_op | source)
XLA Modules:
  0.0 111.8 jit_solution(8905991226627391818)
XLA Ops:
  0.6 109.1 %shard_map.50 = (f32[256,4096]{1,0:T(8,128)S(1)}, f32[2,16,1,128]{3,2,1,0:T(1,128)S(1)}) custom-call(bf16[256,4096]{1,0:T(8,128)(2,1)} %wave.1, bf16[2048,128]{1,0:T(8,128)(2,1)} %eigvec.1, f32[16,128]{1,0:T(8,128)} %bitcast.2), custom_call_target="tpu_custom_call" | custom-call | tf_op jit(solution)/shard_map/pallas_call | solution.py:491
  109.7 2.1 %shard_map.51 = (f32[256,4096]{1,0:T(8,128)}, f32[2,16,1,128]{3,2,1,0:T(1,128)}) custom-call(f32[256,4096]{1,0:T(8,128)S(1)} %get-tuple-element.6.rotated, f32[2,16,1,128]{3,2,1,0:T(1,128)S(1)} %get-tuple-element.7.density), custom_call_target="tpu_custom_call" | custom-call | tf_op jit(solution)/shard_map/pallas_call | solution.py:527

commit v5 on v4

--- a/solution.py
+++ b/solution.py
@@ -35,9 +35,9 @@
 
 def kernel(
     wave, eigvec, occupation, out, density,
-    gathered, away, raw, vectors, seats, weight, staged, passing, part, parts,
+    gathered, away, raw, vectors, seats, weight, staged, passing, part, parts, halves,
     own_in, away_in, raw_in, seats_in, early, late, away_out, peer_out, mate_out, share_out,
-    vec_in, vec_core_in, vec_core, vec_side, vec_mate, res_mate, pass_in, mate_in, side_in, side_out, kept, part_out, part_in,
+    vec_in, vec_core_in, vec_core, vec_side, vec_mate, res_mate, pass_in, mate_in, side_in, side_out, kept, sum_out, sum_in,
 ):
     nb, nz = gathered.shape[1], gathered.shape[1] // 2
     frag, band, slab = (lax.axis_index(name) for name in ("frag", "band", "slab"))
@@ -156,18 +156,21 @@
         own_load(step, i).start()
         return carry
 
+    barrier = pltpu.get_barrier_semaphore()
+    for target in (at(beside), at(mate), at(band, 1 - slab)):
+        pl.semaphore_signal(barrier, inc=1, device_id=target, device_id_type=MESH)
+
+    @pl.when(inner)
+    def _():
+        pl.semaphore_signal(barrier, inc=1, device_id=at(peer), device_id_type=MESH)
+
     for step in range(ahead + 1):
         load(step, None)
     raw_load.start()
     seats_load.start()
 
-    barrier = pltpu.get_barrier_semaphore()
-    for target in (at(beside), at(mate), at(band, 1 - slab)):
-        pl.semaphore_signal(barrier, inc=1, device_id=target, device_id_type=MESH)
-
     @pl.when(inner)
     def _():
-        pl.semaphore_signal(barrier, inc=1, device_id=at(peer), device_id_type=MESH)
         pl.semaphore_wait(barrier, 4)
 
     @pl.when(outer)
@@ -201,9 +204,16 @@
 
     part[...] = jnp.zeros(part.shape, part.dtype)
 
-    def spread(hop):
-        target = lax.rem(band + hop, nb)
-        return send(part, parts.at[band], part_out.at[0], part_in.at[0], at(target))
+    first_steps = pl.ds(0, ahead)
+
+    def sum_to_mate():
+        return send(part.at[first_steps], parts.at[0, first_steps], sum_out.at[0], sum_in.at[0], at(mate))
+
+    def sum_to_peer():
+        return send(part, parts.at[1], sum_out.at[0], sum_in.at[1], at(peer))
+
+    def total_to(b, i):
+        return send(halves.at[x], halves.at[x], sum_out.at[1], sum_in.at[i], at(b))
 
     @pl.when(inner)
     def _():
@@ -304,6 +314,11 @@
                     for p in range(2):
                         to_pass(step, p).start()
 
+                    @pl.when(step == steps - 1)
+                    def _():
+                        for p in range(2):
+                            to_mate_out(step - 1, p).start()
+
                 @pl.when((slot == 1) & (step < steps - 2))
                 def _():
                     for p in range(2):
@@ -351,11 +366,16 @@
             return carry
 
         lax.fori_loop(ahead, steps, body, 0)
-        for hop in range(1, nb):
-            spread(hop).start()
-        for step in (steps - 2, steps - 1):
-            for p in range(2):
-                to_mate_out(step, p).start()
+        settle(parts.at[0, first_steps], sum_in.at[0])
+        part[first_steps] = part[first_steps] + parts[0, first_steps]
+        sum_to_peer().start()
+        settle(parts.at[1], sum_in.at[1])
+        halves[x] = (part[...] + parts[1]) / jnp.float32(total_bands)
+        total_to(mate_beside, 3).start()
+        total_to(mate, 2).start()
+        total_to(beside, 3).start()
+        for p in range(2):
+            to_mate_out(steps - 1, p).start()
 
     @pl.when(outer)
     def _():
@@ -409,8 +429,7 @@
             return carry
 
         lax.fori_loop(0, ahead, shared, 0)
-        for hop in range(1, nb):
-            spread(hop).start()
+        sum_to_mate().start()
 
         def body(step, carry):
             @pl.when(step + 5 < steps)
@@ -428,24 +447,23 @@
             settle(passing.at[steps - 1, tile(p)], pass_in.at[steps - 1 - ahead + p])
             to_side_out(passing.at[steps - 1, tile(p)], steps - 1, p).start()
 
-    parts[band] = part[...]
-    others = parts.at[pl.ds(0, nb - 1)]
-    settle(others, part_in.at[0])
-    for of in range(2):
-        total = parts[of]
-        for level in range(1, nz):
-            total = total + parts[2 * level + of]
-        density[of] = total / jnp.float32(total_bands)
+    @pl.when(outer)
+    def _():
+        settle(halves.at[x], sum_in.at[2])
+
+    settle(halves.at[1 - x], sum_in.at[3])
+    density[...] = halves[...]
 
     def blocks(n):
         return staged.at[pl.ds(0, n // 2), 0]
 
     settle(away, away_out.at[0])
-    settle(others, part_out.at[0])
 
     @pl.when(inner)
     def _():
         settle(gathered.at[pl.ds(0, steps // 2)], peer_out.at[0])
+        settle(part, sum_out.at[0])
+        settle(parts, sum_out.at[1])
         settle(blocks(6 * ahead), share_out.at[0])
         settle(vectors.at[:, pl.ds(0, 4 * width)], vec_core.at[0])
         settle(vectors.at[:, pl.ds(0, 2 * width)], vec_side.at[0])
@@ -454,6 +472,7 @@
 
     @pl.when(outer)
     def _():
+        settle(part.at[first_steps], sum_out.at[0])
         settle(blocks(2 * steps), mate_out.at[0])
         settle(vectors.at[:, pl.ds(0, 2 * width)], vec_core.at[0])
         settle(vectors.at[:, pl.ds(0, width)], vec_side.at[0])
@@ -506,7 +525,8 @@
             pltpu.VMEM((steps, 4, rows, LANES), jnp.float32),
             pltpu.VMEM((steps, rows, LANES), jnp.float32),
             pltpu.VMEM((steps, 1, LANES), jnp.float32),
-            pltpu.VMEM((nb, steps, 1, LANES), jnp.float32),
+            pltpu.VMEM((3, steps, 1, LANES), jnp.float32),
+            pltpu.VMEM((2, steps, 1, LANES), jnp.float32),
             dma((SHARED + 2,)),
             dma((SHARED + 2,)),
             dma((1,)),
@@ -518,7 +538,9 @@
             dma((4,)),
             *[dma((1,))] * 4,
             dma((steps - SHARED + 1,)),
-            *[dma((1,))] * 6,
+            *[dma((1,))] * 4,
+            dma((2,)),
+            dma((4,)),
         ],
         compiler_params=pltpu.CompilerParams(
             collective_id=0, has_side_effects=True, vmem_limit_bytes=56 * 2**20

time: 112 us -> 111 us (level)
  no operation moved by 1% of the time
where the time goes in v5:
time: 111 us
  Pallas kernels  110 us (99%)
    pallas_call x1, Pallas kernels, local(): pl.pallas_call(kernel, out_shape=(pltpu.VMEM((rows, points), jnp.float32)...  108 us

profile of v5, /device:TPU:0, one launch (start us, length us, event | category | flops | bytes accessed | tf_op | source)
XLA Modules:
  0.0 111.1 jit_solution(13358157337603036070)
XLA Ops:
  0.6 108.4 %shard_map.50 = (f32[256,4096]{1,0:T(8,128)S(1)}, f32[2,16,1,128]{3,2,1,0:T(1,128)S(1)}) custom-call(bf16[256,4096]{1,0:T(8,128)(2,1)} %wave.1, bf16[2048,128]{1,0:T(8,128)(2,1)} %eigvec.1, f32[16,128]{1,0:T(8,128)} %bitcast.2), custom_call_target="tpu_custom_call" | custom-call | tf_op jit(solution)/shard_map/pallas_call | solution.py:510
  109.0 2.1 %shard_map.51 = (f32[256,4096]{1,0:T(8,128)}, f32[2,16,1,128]{3,2,1,0:T(1,128)}) custom-call(f32[256,4096]{1,0:T(8,128)S(1)} %get-tuple-element.6.rotated, f32[2,16,1,128]{3,2,1,0:T(1,128)S(1)} %get-tuple-element.7.density), custom_call_target="tpu_custom_call" | custom-call | tf_op jit(solution)/shard_map/pallas_call | solution.py:549

commit v6 on v5

--- a/solution.py
+++ b/solution.py
@@ -281,7 +281,6 @@
         fars(1, (2, 3))
         mate_panel(1)
         mine(5)
-        side(5)
         fars(2, (2, 3))
         mate_panel(2)
         mate_panel(3)
@@ -296,6 +295,7 @@
                 def _():
                     if turn_of == 1:
                         mates(step + 1)
+                        side(step + 2)
                         mine(step + 3)
                         side(step + 3)
                         for q in range(nz):
@@ -332,23 +332,23 @@
             keep(step).start()
             return carry
 
-        lag = ahead + 2
+        lag = ahead + 3
 
         def rows_done(step):
-            return jnp.maximum(step + 1 - lag, 0) + jnp.minimum(jnp.maximum(step - 4, 0) // 2, lag)
+            return jnp.minimum(jnp.maximum(step + 1 - lag, 0) * 5 // 3, steps)
 
         def body(step, carry):
             fars(step)
             for_mate(step)
+
+            @pl.when(step + 2 < steps)
+            def _():
+                mates(step + 2)
 
             @pl.when((step > ahead) & (step + 3 < steps))
             def _():
                 mine(step + 3)
                 side(step + 3)
-
-            @pl.when(step + 2 < steps)
-            def _():
-                mates(step + 2)
 
             @pl.when((step > ahead) & (step + 5 < steps))
             def _():

time: 111 us -> 111 us (level)
  no operation moved by 1% of the time
where the time goes in v6:
time: 111 us
  Pallas kernels  110 us (99%)
    pallas_call x1, Pallas kernels, local(): pl.pallas_call(kernel, out_shape=(pltpu.VMEM((rows, points), jnp.float32)...  108 us

profile of v6, /device:TPU:0, one launch (start us, length us, event | category | flops | bytes accessed | tf_op | source)
XLA Modules:
  0.0 111.1 jit_solution(1687106582085361202)
XLA Ops:
  0.6 108.4 %shard_map.50 = (f32[256,4096]{1,0:T(8,128)S(1)}, f32[2,16,1,128]{3,2,1,0:T(1,128)S(1)}) custom-call(bf16[256,4096]{1,0:T(8,128)(2,1)} %wave.1, bf16[2048,128]{1,0:T(8,128)(2,1)} %eigvec.1, f32[16,128]{1,0:T(8,128)} %bitcast.2), custom_call_target="tpu_custom_call" | custom-call | tf_op jit(solution)/shard_map/pallas_call | solution.py:510
  109.0 2.1 %shard_map.51 = (f32[256,4096]{1,0:T(8,128)}, f32[2,16,1,128]{3,2,1,0:T(1,128)}) custom-call(f32[256,4096]{1,0:T(8,128)S(1)} %get-tuple-element.6.rotated, f32[2,16,1,128]{3,2,1,0:T(1,128)S(1)} %get-tuple-element.7.density), custom_call_target="tpu_custom_call" | custom-call | tf_op jit(solution)/shard_map/pallas_call | solution.py:549

commit v7 on v6

--- a/solution.py
+++ b/solution.py
@@ -151,7 +151,7 @@
         return total
 
     def load(step, carry):
-        i = step if isinstance(step, int) else ahead + 1
+        i = 0 if isinstance(step, int) else 1
         away_load(step, i).start()
         own_load(step, i).start()
         return carry
@@ -178,18 +178,12 @@
         pl.semaphore_wait(barrier, 3)
 
     def exchange(step):
-        if isinstance(step, int) and step <= ahead:
-            away_load(step, step).wait()
         across(step).start()
 
-    def own_ready(step):
-        if isinstance(step, int) and step <= ahead:
-            own_load(step, step).wait()
-
-    def rest_ready():
-        others = pl.ds(ahead + 1, steps - ahead - 1)
-        settle(away.at[others], away_in.at[ahead + 1])
-        settle(away.at[others], own_in.at[ahead + 1])
+    def loaded(i):
+        some = pl.ds(*((0, ahead + 1), (ahead + 1, steps - ahead - 1))[i])
+        settle(away.at[some], away_in.at[i])
+        settle(away.at[some], own_in.at[i])
 
     def turn():
         raw_load.wait()
@@ -225,7 +219,6 @@
                 block(step, b, share_out, mate, 1).start()
 
         def mine(step):
-            own_ready(step)
             onward(step, band)
             share(step, band)
 
@@ -251,6 +244,7 @@
             panel(mate, q, vec_side, beside).start()
             to_core(mate, q).start()
 
+        loaded(0)
         for step in range(ahead):
             mine(step)
             exchange(step)
@@ -259,7 +253,7 @@
         turn()
         for q in range(nz):
             to_core(band, q).start()
-        rest_ready()
+        loaded(1)
         for step in range(4, 8):
             exchange(step)
         panel(band, 0, vec_side, beside).start()
@@ -380,19 +374,19 @@
     @pl.when(outer)
     def _():
         def mine(step):
-            own_ready(step)
             block(step, band, mate_out, mate, 1).start()
 
         def side(step):
             arrived(step, (beside,), 0)
             block(step, beside, mate_out, mate, 1).start()
 
+        loaded(0)
         for step in range(ahead + 1):
             exchange(step)
             mine(step)
         lax.fori_loop(ahead + 1, steps, load, 0)
         turn()
-        rest_ready()
+        loaded(1)
         for step in range(ahead + 1, ahead + 5):
             exchange(step)
         for step in range(ahead + 1):
@@ -527,8 +521,8 @@
             pltpu.VMEM((steps, 1, LANES), jnp.float32),
             pltpu.VMEM((3, steps, 1, LANES), jnp.float32),
             pltpu.VMEM((2, steps, 1, LANES), jnp.float32),
-            dma((SHARED + 2,)),
-            dma((SHARED + 2,)),
+            dma((2,)),
+            dma((2,)),
             dma((1,)),
             dma((1,)),
             dma((SHARED, nb)),

time: 111 us -> 111 us (level)
  no operation moved by 1% of the time
where the time goes in v7:
time: 111 us
  Pallas kernels  110 us (99%)
    pallas_call x1, Pallas kernels, local(): pl.pallas_call(kernel, out_shape=(pltpu.VMEM((rows, points), jnp.float32)...  108 us

profile of v7, /device:TPU:0, one launch (start us, length us, event | category | flops | bytes accessed | tf_op | source)
XLA Modules:
  0.0 111.1 jit_solution(12182863637950610282)
XLA Ops:
  0.6 108.3 %shard_map.50 = (f32[256,4096]{1,0:T(8,128)S(1)}, f32[2,16,1,128]{3,2,1,0:T(1,128)S(1)}) custom-call(bf16[256,4096]{1,0:T(8,128)(2,1)} %wave.1, bf16[2048,128]{1,0:T(8,128)(2,1)} %eigvec.1, f32[16,128]{1,0:T(8,128)} %bitcast.2), custom_call_target="tpu_custom_call" | custom-call | tf_op jit(solution)/shard_map/pallas_call | solution.py:504
  109.0 2.1 %shard_map.51 = (f32[256,4096]{1,0:T(8,128)}, f32[2,16,1,128]{3,2,1,0:T(1,128)}) custom-call(f32[256,4096]{1,0:T(8,128)S(1)} %get-tuple-element.6.rotated, f32[2,16,1,128]{3,2,1,0:T(1,128)S(1)} %get-tuple-element.7.density), custom_call_target="tpu_custom_call" | custom-call | tf_op jit(solution)/shard_map/pallas_call | solution.py:543

commit v8 on v7

--- a/solution.py
+++ b/solution.py
@@ -9,7 +9,7 @@
 
 MESH = pl.DeviceIdType.MESH
 LANES = 128
-PIECES = 8
+PIECES = 2
 SHARED = 3
 
 

time: 111 us -> 111 us (level)
  no operation moved by 1% of the time
where the time goes in v8:
time: 111 us
  Pallas kernels  110 us (99%)
    pallas_call x1, Pallas kernels, local(): pl.pallas_call(kernel, out_shape=(pltpu.VMEM((rows, points), jnp.float32)...  108 us

profile of v8, /device:TPU:0, one launch (start us, length us, event | category | flops | bytes accessed | tf_op | source)
XLA Modules:
  0.0 111.0 jit_solution(14896010536868035903)
XLA Ops:
  0.6 108.3 %shard_map.50 = (f32[256,4096]{1,0:T(8,128)S(1)}, f32[2,16,1,128]{3,2,1,0:T(1,128)S(1)}) custom-call(bf16[256,4096]{1,0:T(8,128)(2,1)} %wave.1, bf16[2048,128]{1,0:T(8,128)(2,1)} %eigvec.1, f32[16,128]{1,0:T(8,128)} %bitcast.2), custom_call_target="tpu_custom_call" | custom-call | tf_op jit(solution)/shard_map/pallas_call | solution.py:504
  109.0 2.0 %shard_map.51 = (f32[256,4096]{1,0:T(8,128)}, f32[2,16,1,128]{3,2,1,0:T(1,128)}) custom-call(f32[256,4096]{1,0:T(8,128)S(1)} %get-tuple-element.6.rotated, f32[2,16,1,128]{3,2,1,0:T(1,128)S(1)} %get-tuple-element.7.density), custom_call_target="tpu_custom_call" | custom-call | tf_op jit(solution)/shard_map/pallas_call | solution.py:543

commit v9 on v8

--- a/solution.py
+++ b/solution.py
@@ -446,7 +446,8 @@
         settle(halves.at[x], sum_in.at[2])
 
     settle(halves.at[1 - x], sum_in.at[3])
-    density[...] = halves[...]
+    density_copy = pltpu.make_async_copy(halves, density, seats_in.at[0])
+    density_copy.start()
 
     def blocks(n):
         return staged.at[pl.ds(0, n // 2), 0]
@@ -476,6 +477,7 @@
 
     settle(blocks(2 * steps), side_out.at[0])
     settle(blocks(2 * steps), side_in.at[0])
+    density_copy.wait()
 
 
 def flush(rotated, density, rotated_out, density_out, sems):
@@ -498,7 +500,6 @@
     if nb != 8 or width != LANES or rows != 2 * width or points % (2 * LANES) or steps < SHARED + 8 or total_bands != nb * rows:
         return plain(wavefunctions, eigvec, occupation)
     nz, deep = nb // 2, total_bands // (nb // 2)
-    vmem = pl.BlockSpec(memory_space=pltpu.VMEM)
     hbm = pl.BlockSpec(memory_space=pltpu.HBM)
     dma = pltpu.SemaphoreType.DMA
     rotated, density = pl.pallas_call(
@@ -508,7 +509,7 @@
             pltpu.VMEM((2, steps, 1, LANES), jnp.float32),
         ),
         in_specs=[hbm] * 3,
-        out_specs=(pl.BlockSpec(memory_space=pl.ANY), vmem),
+        out_specs=[pl.BlockSpec(memory_space=pl.ANY)] * 2,
         scratch_shapes=[
             pltpu.VMEM((steps, nb, rows, LANES), jnp.bfloat16),
             pltpu.VMEM((steps, rows, LANES), jnp.bfloat16),

time: 111 us -> 111 us (level)
  no operation moved by 1% of the time
where the time goes in v9:
time: 111 us
  Pallas kernels  110 us (99%)
    pallas_call x1, Pallas kernels, local(): pl.pallas_call(kernel, out_shape=(pltpu.VMEM((rows, points), jnp.float32)...  108 us

profile of v9, /device:TPU:0, one launch (start us, length us, event | category | flops | bytes accessed | tf_op | source)
XLA Modules:
  0.0 111.0 jit_solution(14795828341217427819)
XLA Ops:
  0.6 108.3 %shard_map.50 = (f32[256,4096]{1,0:T(8,128)S(1)}, f32[2,16,1,128]{3,2,1,0:T(1,128)S(1)}) custom-call(bf16[256,4096]{1,0:T(8,128)(2,1)} %wave.1, bf16[2048,128]{1,0:T(8,128)(2,1)} %eigvec.1, f32[16,128]{1,0:T(8,128)} %bitcast.2), custom_call_target="tpu_custom_call" | custom-call | tf_op jit(solution)/shard_map/pallas_call | solution.py:505
  109.0 2.0 %shard_map.51 = (f32[256,4096]{1,0:T(8,128)}, f32[2,16,1,128]{3,2,1,0:T(1,128)}) custom-call(f32[256,4096]{1,0:T(8,128)S(1)} %get-tuple-element.6.rotated, f32[2,16,1,128]{3,2,1,0:T(1,128)S(1)} %get-tuple-element.7.density), custom_call_target="tpu_custom_call" | custom-call | tf_op jit(solution)/shard_map/pallas_call | solution.py:544
